TPU v7x, 128 devices: a whole 4x4x4 slice. The times are simulated.
128 devices in a mesh: gx: 4 (over y), gy: 4 (over x_lo, core), gz: 8 (over x_hi, z).
Axes of the slice: x: 4 (x_hi: 2, x_lo: 2; x = x_hi * 2 + x_lo), y: 4, z: 4, core: 2. Of those that a mesh axis runs over, the one named last changes fastest.
Arguments:
- phase: int32 [4, 8, 256], P('gx', 'gy', 'gz'), may hold values from 0 to 1
- lame: float32 [2, 2], replicated, may hold values from 0.3 to 10
- start: float32 [3, 32, 16, 32, 1024], P(None, None, 'gx', 'gy', 'gz'), may hold values from -6 to 6
Outputs:
- basis: float32 [3, 32, 16, 32, 1024], P(None, None, 'gx', 'gy', 'gz')
- coarse: float32 [32, 32], replicated
All inputs are finite; a program needn't handle non-finite values.
Results may differ from a plain program's by a relative error of at most 0.0001.
Values sent between devices are 32-bit elements; how exact they have to be, the bound alone decides.
No kernel may reach another device: no remote copies, remote signals or barrier semaphores. Data moves between devices by JAX's collectives and lax.ppermute only.
A program may use at most 64 MiB of HBM per device.

v0:
```python
import functools

import jax
import jax.numpy as jnp
from jax import lax
from jax.experimental import pallas as pl
from jax.experimental.pallas import tpu as pltpu
from jax.sharding import PartitionSpec as P


ITERS = 3
BRICK = 4

COMPS, VECS, NX, NY, NZ = 3, 32, 4, 8, 128
HALF = (COMPS, VECS, NX * NY * NZ // 2)
OUTER, INNER = (0, NX - 1), (1, NX - 2)
F32 = jnp.float32

XI, XLD, XLO, XHD, XHO = 0, 2, 4, 6, 8
YM, YLD, YLO, YHD, YHO = 10, 11, 12, 13, 14
ZLD, ZLO, ZRD, ZRO = 15, 17, 19, 21
KIND = 23
LIMIT = 24 * 1024 * 1024
YCASE = (0, 1, 1, 2, 3, 4, 4, 5)
XCASE = (0, 1, 1, 2)

VMEM = pl.BlockSpec(memory_space=pltpu.VMEM)
SMEM = pl.BlockSpec(memory_space=pltpu.SMEM)


def in_vmem(*arrays):
    return [pltpu.with_memory_space_constraint(a, pltpu.VMEM) for a in arrays]


def lanes():
    return lax.broadcasted_iota(jnp.int32, (VECS, NZ), 1)


def rows(block):
    return pl.ds(pl.multiple_of(block * VECS, VECS), VECS)


def dot_t(a, b):
    return lax.dot_general(
        a, b, (((1,), (1,)), ((), ())), precision=lax.Precision.HIGHEST, preferred_element_type=F32
    )


def dot(a, b):
    return jnp.dot(a, b, precision=lax.Precision.HIGHEST, preferred_element_type=F32)


def block_of(outer, inner, c, xi, yi):
    ref = outer if xi in OUTER else inner
    start = ((xi > 1) * NY + yi) * NZ
    return ref.at[c, :, pl.ds(start, NZ)]


def emit_x(c, xi, yi, value, faces, last):
    x_lo, x_hi = faces
    half = NY // 2
    if not last:
        (x_lo if xi == 0 else x_hi)[rows(c * NY + yi), :] = value
    elif xi == 0 and yi >= half:
        x_lo[rows(c * half + yi - half), :] = value
    elif xi > 0 and yi < half:
        x_hi[rows(c * half + yi), :] = value


def emit_y_z(outer, inner, faces, last):
    lane = lanes()

    def comp(c, carry):
        ends = jnp.zeros((VECS, NZ), F32)
        for xi in range(NX):
            for yi in range(NY):
                value = block_of(outer, inner, c, xi, yi)[...]
                if yi == 0 and not last:
                    faces[1][rows(c * NX + xi), :] = value
                if yi == NY - 1:
                    faces[0][rows(c * NX + xi), :] = value
                b = xi * NY + yi
                if b:
                    value = pltpu.roll(value, 2 * b, 1)
                ends = jnp.where((lane == 2 * b) | (lane == (2 * b - 1) % NZ), value, ends)
        faces[-1][rows(c), :] = ends
        return carry

    lax.fori_loop(0, COMPS, comp, 0)


def node_phases(phase_ref):
    spread = (
        lax.broadcasted_iota(jnp.int32, (NZ // BRICK, NZ), 1) // BRICK
        == lax.broadcasted_iota(jnp.int32, (NZ // BRICK, NZ), 0)
    ).astype(F32)
    bricks = jnp.concatenate([phase_ref[0].astype(F32), jnp.zeros((6, NZ // BRICK), F32)], axis=0)
    return jnp.dot(bricks, spread, preferred_element_type=F32)


def native(xi, yi):
    return pl.ds(xi * NY + yi, VECS, stride=NX * NY)


def pack_outer_kernel(x_ref, phase_ref, nodes_ref, outer, x_lo, x_hi):
    for c in range(COMPS):
        for xi in OUTER:
            for yi in range(NY):
                value = x_ref[pl.ds(c * NX * NY * VECS + xi * NY + yi, VECS, stride=NX * NY), :]
                block_of(outer, None, c, xi, yi)[...] = value
                emit_x(c, xi, yi, value, (x_lo, x_hi), False)
    nodes = node_phases(phase_ref)
    nodes_ref[...] = nodes
    for face in (x_lo, x_hi):
        face[COMPS * NY * VECS : COMPS * NY * VECS + 8, :] = nodes


def pack_inner_kernel(x_ref, nodes_ref, outer, inner, y_hi, y_lo, ends):
    for c in range(COMPS):
        for xi in INNER:
            for yi in range(NY):
                value = x_ref[pl.ds(c * NX * NY * VECS + xi * NY + yi, VECS, stride=NX * NY), :]
                block_of(outer, inner, c, xi, yi)[...] = value
    emit_y_z(outer, inner, (y_hi, y_lo, ends), False)
    for face, blocks in ((y_hi, COMPS * NX), (y_lo, COMPS * NX), (ends, COMPS)):
        face[blocks * VECS : blocks * VECS + 8, :] = nodes_ref[...]


def weight_tables(lame_ref, own_ref, halos, w_ref, d_ref):
    hxm, hxp, hym, hyp, hzm, hzp = halos
    lane = lax.broadcasted_iota(jnp.int32, (1, NZ), 1)
    first = [lax.axis_index(a) == 0 for a in ("gx", "gy", "gz")]
    last = [lax.axis_index(a) == lax.axis_size(a) - 1 for a in ("gx", "gy", "gz")]

    def phases(ref, blocks, outside):
        found = ref[blocks * VECS : blocks * VECS + 8, :]
        found = jnp.where(outside, 0.0, found)
        return [found[j : j + 1] for j in range(2)]

    own = own_ref[...]
    own = [own[j : j + 1] for j in range(2)]
    x_m = phases(hxm, COMPS * NY, first[0])
    x_p = phases(hxp, COMPS * NY, last[0])
    y_m = phases(hym, COMPS * NX, first[1])
    y_p = phases(hyp, COMPS * NX, last[1])
    z_m = phases(hzm, COMPS, first[2])
    z_p = phases(hzp, COMPS, last[2])
    left = [jnp.where(lane == 0, pltpu.roll(z_m[j], 1, 1), pltpu.roll(own[j], 1, 1)) for j in range(2)]
    right = [
        jnp.where(lane == NZ - 1, pltpu.roll(z_p[j], NZ - 1, 1), pltpu.roll(own[j], NZ - 1, 1)) for j in range(2)
    ]
    in_l = jnp.where((lane == 0) & first[2], 0.0, 1.0)
    in_r = jnp.where((lane == NZ - 1) & last[2], 0.0, 1.0)
    in_x = [jnp.where(e[0], 0.0, 1.0) for e in (first, last)]
    in_y = [jnp.where(e[1], 0.0, 1.0) for e in (first, last)]
    tables = []
    for kind in range(2):
        pair = [lame_ref[p, 0] + (lame_ref[p, 0] + lame_ref[p, 1]) if kind else lame_ref[p, 0] for p in range(2)]

        def f(ph):
            return jnp.where(ph > 0.5, pair[1], pair[0])

        table = {}
        for j in range(2):
            here = f(own[j])
            table[XI + j] = here
            table[XLD + j] = 0.5 * (here + f(x_m[j]))
            table[XLO + j] = table[XLD + j] * in_x[0]
            table[XHD + j] = 0.5 * (here + f(x_p[j]))
            table[XHO + j] = table[XHD + j] * in_x[1]
            table[ZLD + j] = 0.5 * (here + f(left[j]))
            table[ZLO + j] = table[ZLD + j] * in_l
            table[ZRD + j] = 0.5 * (here + f(right[j]))
            table[ZRO + j] = table[ZRD + j] * in_r
        table[YM] = 0.5 * (f(own[0]) + f(own[1]))
        table[YLD] = 0.5 * (f(own[0]) + f(y_m[1]))
        table[YLO] = table[YLD] * in_y[0]
        table[YHD] = 0.5 * (f(own[1]) + f(y_p[0]))
        table[YHO] = table[YHD] * in_y[1]
        for row, value in table.items():
            w_ref[kind * KIND + row] = jnp.broadcast_to(value, (8, NZ))
        tables.append(table)
    for c in range(COMPS):
        tx, ty, tz = (tables[1 if c == d else 0] for d in range(3))
        for xc in range(3):
            for yc in range(6):
                j = yc // 3
                along_x = (tx[XLD + j] + tx[XI + j], tx[XI + j] + tx[XI + j], tx[XI + j] + tx[XHD + j])[xc]
                inner = ty[XI + j]
                along_y = (ty[YLD] + inner, inner + inner, inner + ty[YM], ty[YM] + inner, inner + inner, inner + ty[YHD])[yc]
                total = along_x + along_y + (tz[ZLD + j] + tz[ZRD + j])
                d_ref[(c * 3 + xc) * 6 + yc] = jnp.broadcast_to(total, (8, NZ))


def times(weight, value):
    return (weight[None] * value.reshape(4, 8, NZ)).reshape(VECS, NZ)


def kinds(c):
    return [jnp.where(c == d, KIND, 0) for d in range(3)]


def apply_operator(c, outer, inner, halos, w_ref, d_ref, layers, done):
    lane = lanes()
    kx, ky, kz = kinds(c)
    if halos:
        hxm, hxp, hym, hyp, hzm, hzp = halos
        ends = jnp.where(lane % 2 == 0, hzp[rows(c), :], pltpu.roll(hzm[rows(c), :], 2, 1))

    def at(xi, yi):
        return block_of(outer, inner, c, xi, yi)[...]

    for xi in layers:
        for yi in range(NY):
            j = yi // BRICK
            block = xi * NY + yi
            u = at(xi, yi)
            total = times(d_ref[(c * 3 + XCASE[xi]) * 6 + YCASE[yi]], u)
            if xi > 0:
                total -= times(w_ref[kx + XI + j], at(xi - 1, yi))
            elif halos:
                total -= times(w_ref[kx + XLO + j], hxm[rows(c * NY + yi), :])
            if xi < NX - 1:
                total -= times(w_ref[kx + XI + j], at(xi + 1, yi))
            elif halos:
                total -= times(w_ref[kx + XHO + j], hxp[rows(c * NY + yi), :])
            if yi > 0:
                total -= times(w_ref[ky + (YM if yi == BRICK else XI + j)], at(xi, yi - 1))
            elif halos:
                total -= times(w_ref[ky + YLO], hym[rows(c * NX + xi), :])
            if yi < NY - 1:
                total -= times(w_ref[ky + (YM if yi == BRICK - 1 else XI + j)], at(xi, yi + 1))
            elif halos:
                total -= times(w_ref[ky + YHO], hyp[rows(c * NX + xi), :])
            left, right = pltpu.roll(u, 1, 1), pltpu.roll(u, NZ - 1, 1)
            if halos:
                far = pltpu.roll(ends, NZ - 1 - 2 * block, 1)
                left, right = jnp.where(lane == 0, far, left), jnp.where(lane == NZ - 1, far, right)
            else:
                left, right = jnp.where(lane == 0, 0.0, left), jnp.where(lane == NZ - 1, 0.0, right)
            total -= times(w_ref[kz + ZLO + j], left)
            total -= times(w_ref[kz + ZRO + j], right)
            done(xi, yi, total)


def outer_step(w_ref, d_ref, refs, last):
    outer, inner, hxm, hxp, hym, hyp, hzm, hzp, new_outer, x_lo, x_hi = refs

    def comp(c, carry):
        def done(xi, yi, value):
            block_of(new_outer, None, c, xi, yi)[...] = value
            emit_x(c, xi, yi, value, (x_lo, x_hi), last)

        apply_operator(c, outer, inner, (hxm, hxp, hym, hyp, hzm, hzp), w_ref, d_ref, OUTER, done)
        return carry

    lax.fori_loop(0, COMPS, comp, 0)


def first_outer_kernel(lame_ref, nodes_ref, *refs):
    w_ref, d_ref = refs[8:10]
    weight_tables(lame_ref, nodes_ref, refs[2:8], w_ref, d_ref)
    outer_step(w_ref, d_ref, refs[:8] + refs[10:], False)


def outer_kernel(last, w_ref, d_ref, *refs):
    outer_step(w_ref, d_ref, refs, last)


def inner_kernel(last, w_ref, d_ref, outer, inner, hym, hyp, hzm, hzp, new_outer, new_inner, *faces):
    def comp(c, carry):
        def done(xi, yi, value):
            block_of(None, new_inner, c, xi, yi)[...] = value

        apply_operator(c, outer, inner, (None, None, hym, hyp, hzm, hzp), w_ref, d_ref, INNER, done)
        return carry

    lax.fori_loop(0, COMPS, comp, 0)
    emit_y_z(new_outer, new_inner, faces, last)


def gram_kernel(outer, inner, g_ref):
    total = jnp.zeros((VECS, VECS), F32)
    for ref in (outer, inner):
        for c in range(COMPS):
            total += dot_t(ref[c], ref[c])
    g_ref[...] = total


def inside_kernel(w_ref, d_ref, outer, inner, out_ref, pair_ref):
    def comp(c, total):
        def done(xi, yi, value):
            start = (xi * NY + yi) * NZ
            pair_ref[VECS:, start : start + NZ] = value

        apply_operator(c, outer, inner, None, w_ref, d_ref, range(NX), done)
        for xi in range(NX):
            ref, start = (outer if xi in OUTER else inner), (xi > 1) * NY * NZ
            pair_ref[:VECS, xi * NY * NZ : (xi + 1) * NY * NZ] = ref[c, :, start : start + NY * NZ]
        return total + dot_t(pair_ref[:VECS, :], pair_ref[...])

    out_ref[...] = lax.fori_loop(0, COMPS, comp, jnp.zeros((VECS, 2 * VECS), F32))


def across_kernel(w_ref, g1, g2, inside, outer, inner, own_ends, hxm, hxp, hym, hzm, out_ref):
    lane = lanes()
    half = NY // 2

    def comp(c, total):
        kx, ky, kz = kinds(c)
        mine, other = [], []
        for yi in range(NY):
            j = yi // BRICK
            xi = 0 if yi < half else NX - 1
            mine.append(block_of(outer, inner, c, xi, yi)[...])
            halo = hxm if yi < half else hxp
            other.append(times(w_ref[kx + (XLO if yi < half else XHO) + j], halo[rows(c * half + yi % half), :]))
        for xi in range(NX):
            mine.append(block_of(outer, inner, c, xi, 0)[...])
            other.append(times(w_ref[ky + YLO], hym[rows(c * NX + xi), :]))
        weight = [jnp.broadcast_to(w_ref[kz + ZLO + j][:, :1], (8, NZ)) for j in range(2)]
        which = lax.broadcasted_iota(jnp.int32, (8, NZ), 1)
        weight = jnp.where(which // 2 % NY < BRICK, weight[0], weight[1])
        weight = jnp.where((which % 2 == 0) & (which < 2 * NX * NY), weight, 0.0)
        mine.append(own_ends[rows(c), :])
        other.append(times(weight, pltpu.roll(hzm[rows(c), :], 1, 1)))
        return total + dot_t(jnp.concatenate(mine, axis=1), jnp.concatenate(other, axis=1))

    cross = lax.fori_loop(0, COMPS, comp, jnp.zeros((VECS, VECS), F32))
    both = inside[...]
    out_ref[...] = jnp.concatenate([g1[...], g2[...], both[:, :VECS], both[:, VECS:] - 2.0 * cross], axis=1)


def inverse_factor(gram):
    row = lax.broadcasted_iota(jnp.int32, (8, NZ), 0)
    col = lax.broadcasted_iota(jnp.int32, (8, NZ), 1)
    groups = VECS // 8
    cols = []
    for k in range(VECS):
        whole = jnp.broadcast_to(gram[:, k : k + 1], (VECS, NZ))
        cols.append([whole[8 * g : 8 * g + 8] for g in range(groups)])
    unit = [jnp.where(row + 8 * g == col, 1.0, 0.0).astype(F32) for g in range(groups)]

    def spread(group, r):
        return jnp.broadcast_to(group[r : r + 1], (8, NZ))

    for k in range(VECS):
        own, r = divmod(k, 8)
        scale = lax.rsqrt(spread(cols[k][own], r))
        factor = [None] * own + [cols[k][g] * scale for g in range(own, groups)]
        pivot = spread(unit[own], r) * scale
        for j in range(k + 1, VECS):
            at_j = spread(factor[j // 8], j % 8)
            for g in range(j // 8, groups):
                cols[j][g] = cols[j][g] - factor[g] * at_j
        unit[own] = jnp.where(row == r, pivot, jnp.where(row > r, unit[own] - factor[own] * pivot, unit[own]))
        for g in range(own + 1, groups):
            unit[g] = unit[g] - factor[g] * pivot
    return jnp.concatenate(unit, axis=0)[:, :VECS]


def factor_kernel(n_rows, sums_ref, mixing_ref, coarse_ref, grams_ref, turned_ref):
    for k in range(ITERS):
        grams_ref[k] = sums_ref[:, k * VECS : (k + 1) * VECS] / n_rows
    cross = sums_ref[:, ITERS * VECS :] / n_rows
    turned_ref[...] = cross.T
    grams_ref[ITERS] = 0.5 * (cross + turned_ref[...])

    def congruent(k, mixing):
        turned_ref[...] = mixing.T
        return dot(dot(mixing, grams_ref[k]), turned_ref[...])

    mixing = inverse_factor(grams_ref[0])
    for k in range(1, ITERS):
        mixing = dot(inverse_factor(congruent(k, mixing)), mixing)
    coarse_ref[...] = congruent(ITERS, mixing)
    mixing_ref[...] = mixing


def basis_kernel(mixing_ref, outer, inner, basis_ref):
    c = pl.program_id(0)
    for half, layers in ((outer, OUTER), (inner, INNER)):
        value = dot(mixing_ref[...], half[c])
        for slot, xi in enumerate(layers):
            for yi in range(NY):
                start = (slot * NY + yi) * NZ
                basis_ref[native(xi, yi), :] = value[:, start : start + NZ]


def vmem(*shape):
    return pltpu.VMEM(shape, F32)


def faces_x(extra=0, last=False):
    return [vmem(COMPS * NY * VECS // (2 if last else 1) + extra, NZ)] * 2


def faces_y_z(extra=0, last=False):
    return [vmem(COMPS * NX * VECS + extra, NZ)] * (1 if last else 2) + [vmem(COMPS * VECS + extra, NZ)]


def ring(value, axis, by):
    n = lax.axis_size(axis)
    return lax.ppermute(value, axis, [(i, (i + by) % n) for i in range(n)])


def send_x(x_lo, x_hi):
    return in_vmem(ring(x_hi, "gx", 1), ring(x_lo, "gx", -1))


def send_y_z(y_hi, y_lo, ends):
    return in_vmem(ring(y_hi, "gy", 1), ring(y_lo, "gy", -1), ring(ends, "gz", 1), ring(ends, "gz", -1))


def all_sum(value):
    value = value + lax.ppermute(value, "gy", [(i, i ^ 1) for i in range(4)])

    def along_x(by):
        pairs = []
        for i in range(32):
            x_low, core, x_high, z = i // 16, i // 8 % 2, i // 4 % 2, i % 4
            x = (2 * x_high + x_low + by) % 4
            pairs.append((i, (x % 2) * 16 + core * 8 + (x // 2) * 4 + z))
        return pairs

    def along_z(by):
        return [(i, i // 4 * 4 + (i % 4 + by) % 4) for i in range(8)]

    def along_y(by):
        return [(i, (i + by) % 4) for i in range(4)]

    for axis, pairs in ((("gy", "gz"), along_x), ("gx", along_y), ("gz", along_z)):
        one, three, two = (lax.ppermute(value, axis, pairs(by)) for by in (1, 3, 2))
        value = (value + two) + (one + three)
    return value


def call(kernel, outs, args, flops=4_000_000, scratch=(), smem=0):
    return pl.pallas_call(
        kernel,
        out_shape=outs,
        in_specs=[SMEM] * smem + [VMEM] * (len(args) - smem),
        out_specs=jax.tree.map(lambda _: VMEM, outs),
        scratch_shapes=scratch,
        cost_estimate=pl.CostEstimate(flops=flops, bytes_accessed=3_000_000, transcendentals=0),
        compiler_params=pltpu.CompilerParams(vmem_limit_bytes=LIMIT),
    )(*args)


def on_device(phase, lame, start):
    n_rows = 3.0 * start.shape[2] * start.shape[3] * start.shape[4]
    for axis in ("gx", "gy", "gz"):
        n_rows *= lax.axis_size(axis)
    field, small = vmem(*HALF), vmem(VECS, VECS)
    (flat,) = in_vmem(start.reshape(-1, NZ))
    grams = []
    for k in range(ITERS + 1):
        last = k == ITERS
        if k == 0:
            nodes, outer, *x_faces = call(pack_outer_kernel, [vmem(8, NZ), field] + faces_x(8), (flat, phase))
        elif k == 1:
            tables = [vmem(2 * KIND, 8, NZ), vmem(54, 8, NZ)]
            w, d, new_outer, *x_faces = call(
                first_outer_kernel, tables + [field] + faces_x(), (lame, nodes, *old, *x_halos, *halos), smem=1
            )
        else:
            new_outer, *x_faces = call(
                functools.partial(outer_kernel, last), [field] + faces_x(0, last), (w, d, *old, *x_halos, *halos)
            )
        x_halos = send_x(*x_faces)
        if k == 0:
            inner, *faces = call(pack_inner_kernel, [field] + faces_y_z(8), (flat, nodes, outer))
        else:
            outer = new_outer
            inner, *faces = call(
                functools.partial(inner_kernel, last), [field] + faces_y_z(0, last), (w, d, *old, *halos, outer)
            )
        old = in_vmem(outer, inner)
        if not last:
            halos = send_y_z(*faces)
        else:
            y_hi, ends = faces
            halos = in_vmem(ring(y_hi, "gy", 1), ring(ends, "gz", 1))
        if last:
            inside = call(inside_kernel, vmem(VECS, 2 * VECS), (w, d, *old), scratch=[vmem(2 * VECS, NX * NY * NZ)])
        elif k > 0:
            grams.append(call(gram_kernel, small, old))
    sums = call(across_kernel, vmem(VECS, 4 * VECS), (w, *grams, inside, *old, ends, *x_halos, *halos))
    mixing, coarse = call(
        functools.partial(factor_kernel, n_rows),
        [small, jax.ShapeDtypeStruct((VECS, VECS), F32)],
        (all_sum(sums),),
        scratch=[vmem(ITERS + 1, VECS, VECS), vmem(VECS, VECS)],
    )
    rows_of_one = VECS * NX * NY
    basis = pl.pallas_call(
        basis_kernel,
        grid=(COMPS,),
        out_shape=jax.ShapeDtypeStruct((COMPS * rows_of_one, NZ), F32),
        in_specs=[VMEM] * 3,
        out_specs=pl.BlockSpec((rows_of_one, NZ), lambda c: (c, 0)),
        compiler_params=pltpu.CompilerParams(vmem_limit_bytes=LIMIT),
    )(mixing, *old)
    return basis.reshape(start.shape), coarse


def solution(mesh):
    in_specs = (P("gx", "gy", "gz"), P(), P(None, None, "gx", "gy", "gz"))
    out_specs = (P(None, None, "gx", "gy", "gz"), P())
    return jax.shard_map(on_device, mesh=mesh, in_specs=in_specs, out_specs=out_specs, check_vma=False)
```

profile of v0, /device:TPU:4, one launch (start us, length us, event | category | flops | bytes accessed | tf_op | source)
XLA Modules:
  0.0 111.8 jit_solution(10686350462435291964)
XLA Ops:
  7.7 1.7 %collective-permute-start.3 = (f32[392,128]{1,0:T(8,128)S(1)}, f32[392,128]{1,0:T(8,128)S(1)}, u32[]{:S(2)}, u32[]{:S(2)}) collective-permute-start(f32[392,128]{1,0:T(8,128)S(1)} %get-tuple-element.40), channel_id=1, source_target_pairs={{0,24},{8,0},{16,8},{24,16},{1,25},{9,1},{17,9},{25,17},{2,26},{10... | collective-permute-start | bytes 602120 | tf_op jit(solution)/shard_map/ppermute | solution.py:404
  9.4 4.0 %collective-permute-start.5 = (f32[104,128]{1,0:T(8,128)S(1)}, f32[104,128]{1,0:T(8,128)S(1)}, u32[]{:S(2)}, u32[]{:S(2)}) collective-permute-start(f32[104,128]{1,0:T(8,128)S(1)} %get-tuple-element.41), channel_id=1, source_target_pairs={{0,7},{1,0},{2,1},{3,2},{4,3},{5,4},{6,5},{7,6},{8,15},{9,8},{10,9... | collective-permute-start | bytes 159752 | tf_op jit(solution)/shard_map/ppermute | solution.py:404
  13.4 1.8 %collective-permute-done.5.refs_7_.hzp = f32[104,128]{1,0:T(8,128)S(1)} collective-permute-done((f32[104,128]{1,0:T(8,128)S(1)}, f32[104,128]{1,0:T(8,128)S(1)}, u32[]{:S(2)}, u32[]{:S(2)}) %collective-permute-start.5) | collective-permute-done | bytes 53280 | tf_op jit(solution)/shard_map/ppermute | solution.py:404
  15.5 7.8 %collective-permute-done.4.refs_6_.hzm = f32[104,128]{1,0:T(8,128)S(1)} collective-permute-done((f32[104,128]{1,0:T(8,128)S(1)}, f32[104,128]{1,0:T(8,128)S(1)}, u32[]{:S(2)}, u32[]{:S(2)}) %collective-permute-start.4) | collective-permute-done | bytes 53280 | tf_op jit(solution)/shard_map/ppermute | solution.py:404
  25.3 2.9 %collective-permute-start.7 = (f32[768,128]{1,0:T(8,128)S(1)}, f32[768,128]{1,0:T(8,128)S(1)}, u32[]{:S(2)}, u32[]{:S(2)}) collective-permute-start(f32[768,128]{1,0:T(8,128)S(1)} %get-tuple-element.47), channel_id=1, source_target_pairs={{0,96},{32,0},{64,32},{96,64},{1,97},{33,1},{65,33},{97,65},{2,98}... | collective-permute-start | bytes 1179656 | tf_op jit(solution)/shard_map/ppermute | solution.py:404
  29.8 1.7 %collective-permute-start.9 = (f32[384,128]{1,0:T(8,128)S(1)}, f32[384,128]{1,0:T(8,128)S(1)}, u32[]{:S(2)}, u32[]{:S(2)}) collective-permute-start(f32[384,128]{1,0:T(8,128)S(1)} %get-tuple-element.49), channel_id=1, source_target_pairs={{0,24},{8,0},{16,8},{24,16},{1,25},{9,1},{17,9},{25,17},{2,26},{10... | collective-permute-start | bytes 589832 | tf_op jit(solution)/shard_map/ppermute | solution.py:404
  31.5 2.0 %collective-permute-start.11 = (f32[96,128]{1,0:T(8,128)S(1)}, f32[96,128]{1,0:T(8,128)S(1)}, u32[]{:S(2)}, u32[]{:S(2)}) collective-permute-start(f32[96,128]{1,0:T(8,128)S(1)} %get-tuple-element.50), channel_id=1, source_target_pairs={{0,7},{1,0},{2,1},{3,2},{4,3},{5,4},{6,5},{7,6},{8,15},{9,8},{10,9... | collective-permute-start | bytes 147464 | tf_op jit(solution)/shard_map/ppermute | solution.py:404
  33.5 4.1 %collective-permute-done.11.refs_7_.hzp = f32[96,128]{1,0:T(8,128)S(1)} collective-permute-done((f32[96,128]{1,0:T(8,128)S(1)}, f32[96,128]{1,0:T(8,128)S(1)}, u32[]{:S(2)}, u32[]{:S(2)}) %collective-permute-start.11) | collective-permute-done | bytes 49184 | tf_op jit(solution)/shard_map/ppermute | solution.py:404
  37.6 8.2 %collective-permute-done.10.refs_6_.hzm = f32[96,128]{1,0:T(8,128)S(1)} collective-permute-done((f32[96,128]{1,0:T(8,128)S(1)}, f32[96,128]{1,0:T(8,128)S(1)}, u32[]{:S(2)}, u32[]{:S(2)}) %collective-permute-start.10) | collective-permute-done | bytes 49184 | tf_op jit(solution)/shard_map/ppermute | solution.py:404
  46.8 3.2 %collective-permute-start.13 = (f32[768,128]{1,0:T(8,128)S(1)}, f32[768,128]{1,0:T(8,128)S(1)}, u32[]{:S(2)}, u32[]{:S(2)}) collective-permute-start(f32[768,128]{1,0:T(8,128)S(1)} %get-tuple-element.54), channel_id=1, source_target_pairs={{0,96},{32,0},{64,32},{96,64},{1,97},{33,1},{65,33},{97,65},{2,98}... | collective-permute-start | bytes 1179656 | tf_op jit(solution)/shard_map/ppermute | solution.py:404
  53.3 2.0 %collective-permute-start.17 = (f32[96,128]{1,0:T(8,128)S(1)}, f32[96,128]{1,0:T(8,128)S(1)}, u32[]{:S(2)}, u32[]{:S(2)}) collective-permute-start(f32[96,128]{1,0:T(8,128)S(1)} %get-tuple-element.57), channel_id=1, source_target_pairs={{0,7},{1,0},{2,1},{3,2},{4,3},{5,4},{6,5},{7,6},{8,15},{9,8},{10,9... | collective-permute-start | bytes 147464 | tf_op jit(solution)/shard_map/ppermute | solution.py:404
  55.3 2.2 %collective-permute-done.17.refs_7_.hzp = f32[96,128]{1,0:T(8,128)S(1)} collective-permute-done((f32[96,128]{1,0:T(8,128)S(1)}, f32[96,128]{1,0:T(8,128)S(1)}, u32[]{:S(2)}, u32[]{:S(2)}) %collective-permute-start.17) | collective-permute-done | bytes 49184 | tf_op jit(solution)/shard_map/ppermute | solution.py:404
  57.5 8.2 %collective-permute-done.16.refs_6_.hzm = f32[96,128]{1,0:T(8,128)S(1)} collective-permute-done((f32[96,128]{1,0:T(8,128)S(1)}, f32[96,128]{1,0:T(8,128)S(1)}, u32[]{:S(2)}, u32[]{:S(2)}) %collective-permute-start.16) | collective-permute-done | bytes 49184 | tf_op jit(solution)/shard_map/ppermute | solution.py:404
  66.7 3.2 %collective-permute-start.19 = (f32[384,128]{1,0:T(8,128)S(1)}, f32[384,128]{1,0:T(8,128)S(1)}, u32[]{:S(2)}, u32[]{:S(2)}) collective-permute-start(f32[384,128]{1,0:T(8,128)S(1)} %get-tuple-element.62), channel_id=1, source_target_pairs={{0,96},{32,0},{64,32},{96,64},{1,97},{33,1},{65,33},{97,65},{2,98}... | collective-permute-start | bytes 589832 | tf_op jit(solution)/shard_map/ppermute | solution.py:404
  74.5 3.2 %shard_map.60.inside = f32[32,64]{1,0:T(8,128)S(1)} custom-call(f32[46,8,128]{2,1,0:T(8,128)S(1)} %get-tuple-element.42.w_ref, f32[54,8,128]{2,1,0:T(8,128)S(1)} %get-tuple-element.44.d_ref, f32[3,32,2048]{2,1,0:T(8,128)S(1)} %get-tuple-element.58.new_outer.outer, f32[3,32,2048]{2,1,0:T(8,128)S(1)} %get-tuple-element.59.inner), custom_call_target="tpu_custom_call" | custom-call | flops 4000000 | bytes 3000000 | tf_op jit(solution)/shard_map/pallas_call | solution.py:439
  77.7 1.8 %collective-permute-done.21.hzm = f32[96,128]{1,0:T(8,128)S(1)} collective-permute-done((f32[96,128]{1,0:T(8,128)S(1)}, f32[96,128]{1,0:T(8,128)S(1)}, u32[]{:S(2)}, u32[]{:S(2)}) %collective-permute-start.21) | collective-permute-done | bytes 49184 | tf_op jit(solution)/shard_map/ppermute | solution.py:404
  82.1 1.9 %collective-permute-start.25 = (f32[32,128]{1,0:T(8,128)S(1)}, f32[32,128]{1,0:T(8,128)S(1)}, u32[]{:S(2)}, u32[]{:S(2)}) collective-permute-start(f32[32,128]{1,0:T(8,128)S(1)} %add.30), channel_id=1, source_target_pairs={{0,20},{1,21},{2,22},{3,23},{4,16},{5,17},{6,18},{7,19},{8,28},{9,... | collective-permute-start | bytes 49160 | tf_op jit(solution)/shard_map/ppermute | solution.py:433
  84.1 2.6 %collective-permute-start.23 = (f32[32,128]{1,0:T(8,128)S(1)}, f32[32,128]{1,0:T(8,128)S(1)}, u32[]{:S(2)}, u32[]{:S(2)}) collective-permute-start(f32[32,128]{1,0:T(8,128)S(1)} %add.30), channel_id=1, source_target_pairs={{0,4},{1,5},{2,6},{3,7},{4,0},{5,1},{6,2},{7,3},{8,12},{9,13},{10,... | collective-permute-start | bytes 49160 | tf_op jit(solution)/shard_map/ppermute | solution.py:433
  89.4 2.0 %collective-permute-start.27 = (f32[32,128]{1,0:T(8,128)S(1)}, f32[32,128]{1,0:T(8,128)S(1)}, u32[]{:S(2)}, u32[]{:S(2)}) collective-permute-start(f32[32,128]{1,0:T(8,128)S(1)} %add_add_fusion.2), channel_id=1, source_target_pairs={{0,32},{32,64},{64,96},{96,0},{1,33},{33,65},{65,97},{97,1},{2,34}... | collective-permute-start | bytes 49160 | tf_op jit(solution)/shard_map/ppermute | solution.py:433
  94.4 2.2 %collective-permute-done.26 = f32[32,128]{1,0:T(8,128)S(1)} collective-permute-done((f32[32,128]{1,0:T(8,128)S(1)}, f32[32,128]{1,0:T(8,128)S(1)}, u32[]{:S(2)}, u32[]{:S(2)}) %collective-permute-start.26) | collective-permute-done | bytes 16416 | tf_op jit(solution)/shard_map/ppermute | solution.py:433
  96.7 3.6 %collective-permute-start.31 = (f32[32,128]{1,0:T(8,128)S(1)}, f32[32,128]{1,0:T(8,128)S(1)}, u32[]{:S(2)}, u32[]{:S(2)}) collective-permute-start(f32[32,128]{1,0:T(8,128)S(1)} %add_add_fusion.1), channel_id=1, source_target_pairs={{0,3},{1,0},{2,1},{3,2},{4,7},{5,4},{6,5},{7,6},{8,11},{9,8},{10,9... | collective-permute-start | bytes 49160 | tf_op jit(solution)/shard_map/ppermute | solution.py:433
  101.8 3.4 %collective-permute-done.30 = f32[32,128]{1,0:T(8,128)S(1)} collective-permute-done((f32[32,128]{1,0:T(8,128)S(1)}, f32[32,128]{1,0:T(8,128)S(1)}, u32[]{:S(2)}, u32[]{:S(2)}) %collective-permute-start.30) | collective-permute-done | bytes 16416 | tf_op jit(solution)/shard_map/ppermute | solution.py:433
  105.5 3.5 %shard_map.62 = (f32[32,32]{1,0:T(8,128)S(1)}, f32[32,32]{1,0:T(8,128)}) custom-call(f32[32,128]{1,0:T(8,128)S(1)} %add_add_fusion.sums_ref), custom_call_target="tpu_custom_call" | custom-call | flops 4000000 | bytes 3000000 | tf_op jit(solution)/shard_map/pallas_call | solution.py:439
  109.0 2.8 %shard_map.63 = f32[3072,128]{1,0:T(8,128)} custom-call(f32[32,32]{1,0:T(8,128)S(1)} %get-tuple-element.64.mixing_ref, f32[3,32,2048]{2,1,0:T(8,128)S(1)} %get-tuple-element.58.new_outer.outer, f32[3,32,2048]{2,1,0:T(8,128)S(1)} %get-tuple-element.59.inner), custom_call_target="tpu_custom_call" | custom-call | tf_op jit(solution)/shard_map/pallas_call | solution.py:496
  (64 shorter events, 31.1 us)
Async XLA Ops:
  3.3 20.0 %collective-permute-start = (f32[776,128]{1,0:T(8,128)S(1)}, f32[776,128]{1,0:T(8,128)S(1)}, u32[]{:S(2)}, u32[]{:S(2)}) collective-permute-start(f32[776,128]{1,0:T(8,128)S(1)} %get-tuple-element.37), channel_id=1, source_target_pairs={{0,32},{32,64},{64,96},{96,0},{1,33},{33,65},{65,97},{97,1},{2,34}... | collective-permute-start | bytes 1191944 | tf_op jit(solution)/shard_map/ppermute | solution.py:404
  4.9 18.4 %collective-permute-start.1 = (f32[776,128]{1,0:T(8,128)S(1)}, f32[776,128]{1,0:T(8,128)S(1)}, u32[]{:S(2)}, u32[]{:S(2)}) collective-permute-start(f32[776,128]{1,0:T(8,128)S(1)} %get-tuple-element.38), channel_id=1, source_target_pairs={{0,96},{32,0},{64,32},{96,64},{1,97},{33,1},{65,33},{97,65},{2,98}... | collective-permute-start | bytes 1191944 | tf_op jit(solution)/shard_map/ppermute | solution.py:404
  7.6 15.7 %collective-permute-start.2 = (f32[392,128]{1,0:T(8,128)S(1)}, f32[392,128]{1,0:T(8,128)S(1)}, u32[]{:S(2)}, u32[]{:S(2)}) collective-permute-start(f32[392,128]{1,0:T(8,128)S(1)} %get-tuple-element.39), channel_id=1, source_target_pairs={{0,8},{8,16},{16,24},{24,0},{1,9},{9,17},{17,25},{25,1},{2,10},{10... | collective-permute-start | bytes 602120 | tf_op jit(solution)/shard_map/ppermute | solution.py:404
  7.7 15.6 %collective-permute-start.3 = (f32[392,128]{1,0:T(8,128)S(1)}, f32[392,128]{1,0:T(8,128)S(1)}, u32[]{:S(2)}, u32[]{:S(2)}) collective-permute-start(f32[392,128]{1,0:T(8,128)S(1)} %get-tuple-element.40), channel_id=1, source_target_pairs={{0,24},{8,0},{16,8},{24,16},{1,25},{9,1},{17,9},{25,17},{2,26},{10... | collective-permute-start | bytes 602120 | tf_op jit(solution)/shard_map/ppermute | solution.py:404
  9.4 5.8 %collective-permute-start.5 = (f32[104,128]{1,0:T(8,128)S(1)}, f32[104,128]{1,0:T(8,128)S(1)}, u32[]{:S(2)}, u32[]{:S(2)}) collective-permute-start(f32[104,128]{1,0:T(8,128)S(1)} %get-tuple-element.41), channel_id=1, source_target_pairs={{0,7},{1,0},{2,1},{3,2},{4,3},{5,4},{6,5},{7,6},{8,15},{9,8},{10,9... | collective-permute-start | bytes 159752 | tf_op jit(solution)/shard_map/ppermute | solution.py:404
  15.2 8.1 %collective-permute-start.4 = (f32[104,128]{1,0:T(8,128)S(1)}, f32[104,128]{1,0:T(8,128)S(1)}, u32[]{:S(2)}, u32[]{:S(2)}) collective-permute-start(f32[104,128]{1,0:T(8,128)S(1)} %get-tuple-element.41), channel_id=1, source_target_pairs={{0,1},{1,2},{2,3},{3,4},{4,5},{5,6},{6,7},{7,0},{8,9},{9,10},{10,1... | collective-permute-start | bytes 159752 | tf_op jit(solution)/shard_map/ppermute | solution.py:404
  24.9 20.9 %collective-permute-start.6 = (f32[768,128]{1,0:T(8,128)S(1)}, f32[768,128]{1,0:T(8,128)S(1)}, u32[]{:S(2)}, u32[]{:S(2)}) collective-permute-start(f32[768,128]{1,0:T(8,128)S(1)} %get-tuple-element.46), channel_id=1, source_target_pairs={{0,32},{32,64},{64,96},{96,0},{1,33},{33,65},{65,97},{97,1},{2,34}... | collective-permute-start | bytes 1179656 | tf_op jit(solution)/shard_map/ppermute | solution.py:404
  25.3 20.5 %collective-permute-start.7 = (f32[768,128]{1,0:T(8,128)S(1)}, f32[768,128]{1,0:T(8,128)S(1)}, u32[]{:S(2)}, u32[]{:S(2)}) collective-permute-start(f32[768,128]{1,0:T(8,128)S(1)} %get-tuple-element.47), channel_id=1, source_target_pairs={{0,96},{32,0},{64,32},{96,64},{1,97},{33,1},{65,33},{97,65},{2,98}... | collective-permute-start | bytes 1179656 | tf_op jit(solution)/shard_map/ppermute | solution.py:404
  29.7 16.1 %collective-permute-start.8 = (f32[384,128]{1,0:T(8,128)S(1)}, f32[384,128]{1,0:T(8,128)S(1)}, u32[]{:S(2)}, u32[]{:S(2)}) collective-permute-start(f32[384,128]{1,0:T(8,128)S(1)} %get-tuple-element.48), channel_id=1, source_target_pairs={{0,8},{8,16},{16,24},{24,0},{1,9},{9,17},{17,25},{25,1},{2,10},{10... | collective-permute-start | bytes 589832 | tf_op jit(solution)/shard_map/ppermute | solution.py:404
  29.8 16.0 %collective-permute-start.9 = (f32[384,128]{1,0:T(8,128)S(1)}, f32[384,128]{1,0:T(8,128)S(1)}, u32[]{:S(2)}, u32[]{:S(2)}) collective-permute-start(f32[384,128]{1,0:T(8,128)S(1)} %get-tuple-element.49), channel_id=1, source_target_pairs={{0,24},{8,0},{16,8},{24,16},{1,25},{9,1},{17,9},{25,17},{2,26},{10... | collective-permute-start | bytes 589832 | tf_op jit(solution)/shard_map/ppermute | solution.py:404
  31.5 6.1 %collective-permute-start.11 = (f32[96,128]{1,0:T(8,128)S(1)}, f32[96,128]{1,0:T(8,128)S(1)}, u32[]{:S(2)}, u32[]{:S(2)}) collective-permute-start(f32[96,128]{1,0:T(8,128)S(1)} %get-tuple-element.50), channel_id=1, source_target_pairs={{0,7},{1,0},{2,1},{3,2},{4,3},{5,4},{6,5},{7,6},{8,15},{9,8},{10,9... | collective-permute-start | bytes 147464 | tf_op jit(solution)/shard_map/ppermute | solution.py:404
  37.6 8.2 %collective-permute-start.10 = (f32[96,128]{1,0:T(8,128)S(1)}, f32[96,128]{1,0:T(8,128)S(1)}, u32[]{:S(2)}, u32[]{:S(2)}) collective-permute-start(f32[96,128]{1,0:T(8,128)S(1)} %get-tuple-element.50), channel_id=1, source_target_pairs={{0,1},{1,2},{2,3},{3,4},{4,5},{5,6},{6,7},{7,0},{8,9},{9,10},{10,1... | collective-permute-start | bytes 147464 | tf_op jit(solution)/shard_map/ppermute | solution.py:404
  46.7 19.0 %collective-permute-start.12 = (f32[768,128]{1,0:T(8,128)S(1)}, f32[768,128]{1,0:T(8,128)S(1)}, u32[]{:S(2)}, u32[]{:S(2)}) collective-permute-start(f32[768,128]{1,0:T(8,128)S(1)} %get-tuple-element.53), channel_id=1, source_target_pairs={{0,32},{32,64},{64,96},{96,0},{1,33},{33,65},{65,97},{97,1},{2,34}... | collective-permute-start | bytes 1179656 | tf_op jit(solution)/shard_map/ppermute | solution.py:404
  46.8 18.9 %collective-permute-start.13 = (f32[768,128]{1,0:T(8,128)S(1)}, f32[768,128]{1,0:T(8,128)S(1)}, u32[]{:S(2)}, u32[]{:S(2)}) collective-permute-start(f32[768,128]{1,0:T(8,128)S(1)} %get-tuple-element.54), channel_id=1, source_target_pairs={{0,96},{32,0},{64,32},{96,64},{1,97},{33,1},{65,33},{97,65},{2,98}... | collective-permute-start | bytes 1179656 | tf_op jit(solution)/shard_map/ppermute | solution.py:404
  51.5 14.2 %collective-permute-start.14 = (f32[384,128]{1,0:T(8,128)S(1)}, f32[384,128]{1,0:T(8,128)S(1)}, u32[]{:S(2)}, u32[]{:S(2)}) collective-permute-start(f32[384,128]{1,0:T(8,128)S(1)} %get-tuple-element.55), channel_id=1, source_target_pairs={{0,8},{8,16},{16,24},{24,0},{1,9},{9,17},{17,25},{25,1},{2,10},{10... | collective-permute-start | bytes 589832 | tf_op jit(solution)/shard_map/ppermute | solution.py:404
  51.6 14.1 %collective-permute-start.15 = (f32[384,128]{1,0:T(8,128)S(1)}, f32[384,128]{1,0:T(8,128)S(1)}, u32[]{:S(2)}, u32[]{:S(2)}) collective-permute-start(f32[384,128]{1,0:T(8,128)S(1)} %get-tuple-element.56), channel_id=1, source_target_pairs={{0,24},{8,0},{16,8},{24,16},{1,25},{9,1},{17,9},{25,17},{2,26},{10... | collective-permute-start | bytes 589832 | tf_op jit(solution)/shard_map/ppermute | solution.py:404
  57.5 8.2 %collective-permute-start.16 = (f32[96,128]{1,0:T(8,128)S(1)}, f32[96,128]{1,0:T(8,128)S(1)}, u32[]{:S(2)}, u32[]{:S(2)}) collective-permute-start(f32[96,128]{1,0:T(8,128)S(1)} %get-tuple-element.57), channel_id=1, source_target_pairs={{0,1},{1,2},{2,3},{3,4},{4,5},{5,6},{6,7},{7,0},{8,9},{9,10},{10,1... | collective-permute-start | bytes 147464 | tf_op jit(solution)/shard_map/ppermute | solution.py:404
  66.6 12.9 %collective-permute-start.18 = (f32[384,128]{1,0:T(8,128)S(1)}, f32[384,128]{1,0:T(8,128)S(1)}, u32[]{:S(2)}, u32[]{:S(2)}) collective-permute-start(f32[384,128]{1,0:T(8,128)S(1)} %get-tuple-element.61), channel_id=1, source_target_pairs={{0,32},{32,64},{64,96},{96,0},{1,33},{33,65},{65,97},{97,1},{2,34}... | collective-permute-start | bytes 589832 | tf_op jit(solution)/shard_map/ppermute | solution.py:404
  66.7 12.8 %collective-permute-start.19 = (f32[384,128]{1,0:T(8,128)S(1)}, f32[384,128]{1,0:T(8,128)S(1)}, u32[]{:S(2)}, u32[]{:S(2)}) collective-permute-start(f32[384,128]{1,0:T(8,128)S(1)} %get-tuple-element.62), channel_id=1, source_target_pairs={{0,96},{32,0},{64,32},{96,64},{1,97},{33,1},{65,33},{97,65},{2,98}... | collective-permute-start | bytes 589832 | tf_op jit(solution)/shard_map/ppermute | solution.py:404
  71.4 8.0 %collective-permute-start.20 = (f32[384,128]{1,0:T(8,128)S(1)}, f32[384,128]{1,0:T(8,128)S(1)}, u32[]{:S(2)}, u32[]{:S(2)}) collective-permute-start(f32[384,128]{1,0:T(8,128)S(1)} %get-tuple-element.63), channel_id=1, source_target_pairs={{0,8},{8,16},{16,24},{24,0},{1,9},{9,17},{17,25},{25,1},{2,10},{10... | collective-permute-start | bytes 589832 | tf_op jit(solution)/shard_map/ppermute | solution.py:404
  71.5 8.0 %collective-permute-start.21 = (f32[96,128]{1,0:T(8,128)S(1)}, f32[96,128]{1,0:T(8,128)S(1)}, u32[]{:S(2)}, u32[]{:S(2)}) collective-permute-start(f32[96,128]{1,0:T(8,128)S(1)} %get-tuple-element.60.own_ends), channel_id=1, source_target_pairs={{0,1},{1,2},{2,3},{3,4},{4,5},{5,6},{6,7},{7,0},{8,9},{9,10},{10,1... | collective-permute-start | bytes 147464 | tf_op jit(solution)/shard_map/ppermute | solution.py:404
  84.1 5.2 %collective-permute-start.23 = (f32[32,128]{1,0:T(8,128)S(1)}, f32[32,128]{1,0:T(8,128)S(1)}, u32[]{:S(2)}, u32[]{:S(2)}) collective-permute-start(f32[32,128]{1,0:T(8,128)S(1)} %add.30), channel_id=1, source_target_pairs={{0,4},{1,5},{2,6},{3,7},{4,0},{5,1},{6,2},{7,3},{8,12},{9,13},{10,... | collective-permute-start | bytes 49160 | tf_op jit(solution)/shard_map/ppermute | solution.py:433
  91.4 5.2 %collective-permute-start.26 = (f32[32,128]{1,0:T(8,128)S(1)}, f32[32,128]{1,0:T(8,128)S(1)}, u32[]{:S(2)}, u32[]{:S(2)}) collective-permute-start(f32[32,128]{1,0:T(8,128)S(1)} %add_add_fusion.2), channel_id=1, source_target_pairs={{0,64},{32,96},{64,0},{96,32},{1,65},{33,97},{65,1},{97,33},{2,66}... | collective-permute-start | bytes 49160 | tf_op jit(solution)/shard_map/ppermute | solution.py:433
  100.2 5.2 %collective-permute-start.29 = (f32[32,128]{1,0:T(8,128)S(1)}, f32[32,128]{1,0:T(8,128)S(1)}, u32[]{:S(2)}, u32[]{:S(2)}) collective-permute-start(f32[32,128]{1,0:T(8,128)S(1)} %add_add_fusion.1), channel_id=1, source_target_pairs={{0,2},{1,3},{2,0},{3,1},{4,6},{5,7},{6,4},{7,5},{8,10},{9,11},{10,... | collective-permute-start | bytes 49160 | tf_op jit(solution)/shard_map/ppermute | solution.py:433
  (11 other events, 54.9 us)
where the time goes:
time: 114 us; the launch traced here: 112 us
  waiting for transfers between devices  46.4 us (41%)
  starting transfers between devices  39.6 us (35%)
  Pallas kernels  22.8 us (20%)
  local copies, waits for them, and re-layouts  2.08 us (2%)
    ppermute x22, waiting for transfers between devices, ring(): return lax.ppermute(value, axis, [(i, (i + by) % n) for i in range(n)])  34 us
    ppermute x22, starting transfers between devices, ring(): return lax.ppermute(value, axis, [(i, (i + by) % n) for i in range(n)])  27.2 us
    pallas_call x13, Pallas kernels, call(): pl.pallas_call(kernel, out_shape=outs, in_specs=[SMEM] * smem + [VMEM] *...  20.1 us
    ppermute x9, starting transfers between devices, all_sum(): one, three, two = (lax.ppermute(value, axis, pairs(by)) for by in (1, 3, 2))  11.8 us
    ppermute x9, waiting for transfers between devices, all_sum(): one, three, two = (lax.ppermute(value, axis, pairs(by)) for by in (1, 3, 2))  11.6 us
    pallas_call x1, Pallas kernels, on_device(): pl.pallas_call(basis_kernel, grid=(COMPS,), out_shape=jax.ShapeDtypeStruc...  2.77 us
  transfers between devices with their start and end apart: 32, of which 15 were waited for; matrix products, arithmetic and copies ran while one was open for 0% of the time, Pallas kernels for 10%

commit v1 on v0

--- a/solution.py
+++ b/solution.py
@@ -430,7 +430,10 @@
         return [(i, (i + by) % 4) for i in range(4)]
 
     for axis, pairs in ((("gy", "gz"), along_x), ("gx", along_y), ("gz", along_z)):
-        one, three, two = (lax.ppermute(value, axis, pairs(by)) for by in (1, 3, 2))
+        parts = []
+        for by in (1, 2, 3):
+            parts.append(lax.ppermute(value, axis, pairs(by)))
+        one, two, three = parts
         value = (value + two) + (one + three)
     return value
 

time: 114 us -> 114 us (level)
  no operation moved by 1% of the time
where the time goes in v1:
time: 114 us; the launch traced here: 112 us
  waiting for transfers between devices  46.4 us (41%)
  starting transfers between devices  39.6 us (35%)
  Pallas kernels  22.8 us (20%)
  local copies, waits for them, and re-layouts  2.08 us (2%)
    ppermute x22, waiting for transfers between devices, ring(): return lax.ppermute(value, axis, [(i, (i + by) % n) for i in range(n)])  34 us
    ppermute x22, starting transfers between devices, ring(): return lax.ppermute(value, axis, [(i, (i + by) % n) for i in range(n)])  27.2 us
    pallas_call x13, Pallas kernels, call(): pl.pallas_call(kernel, out_shape=outs, in_specs=[SMEM] * smem + [VMEM] *...  20.1 us
    ppermute x9, starting transfers between devices, all_sum(): parts.append(lax.ppermute(value, axis, pairs(by)))  11.8 us
    ppermute x9, waiting for transfers between devices, all_sum(): parts.append(lax.ppermute(value, axis, pairs(by)))  11.6 us
    pallas_call x1, Pallas kernels, on_device(): pl.pallas_call(basis_kernel, grid=(COMPS,), out_shape=jax.ShapeDtypeStruc...  2.77 us
  transfers between devices with their start and end apart: 32, of which 15 were waited for; matrix products, arithmetic and copies ran while one was open for 0% of the time, Pallas kernels for 10%

profile of v1, /device:TPU:4, one launch (start us, length us, event | category | flops | bytes accessed | tf_op | source)
XLA Modules:
  0.0 111.8 jit_solution(10686350462435291964)
XLA Ops:
  7.7 1.7 %collective-permute-start.3 = (f32[392,128]{1,0:T(8,128)S(1)}, f32[392,128]{1,0:T(8,128)S(1)}, u32[]{:S(2)}, u32[]{:S(2)}) collective-permute-start(f32[392,128]{1,0:T(8,128)S(1)} %get-tuple-element.40), channel_id=1, source_target_pairs={{0,24},{8,0},{16,8},{24,16},{1,25},{9,1},{17,9},{25,17},{2,26},{10... | collective-permute-start | bytes 602120 | tf_op jit(solution)/shard_map/ppermute | solution.py:404
  9.4 4.0 %collective-permute-start.5 = (f32[104,128]{1,0:T(8,128)S(1)}, f32[104,128]{1,0:T(8,128)S(1)}, u32[]{:S(2)}, u32[]{:S(2)}) collective-permute-start(f32[104,128]{1,0:T(8,128)S(1)} %get-tuple-element.41), channel_id=1, source_target_pairs={{0,7},{1,0},{2,1},{3,2},{4,3},{5,4},{6,5},{7,6},{8,15},{9,8},{10,9... | collective-permute-start | bytes 159752 | tf_op jit(solution)/shard_map/ppermute | solution.py:404
  13.4 1.8 %collective-permute-done.5.refs_7_.hzp = f32[104,128]{1,0:T(8,128)S(1)} collective-permute-done((f32[104,128]{1,0:T(8,128)S(1)}, f32[104,128]{1,0:T(8,128)S(1)}, u32[]{:S(2)}, u32[]{:S(2)}) %collective-permute-start.5) | collective-permute-done | bytes 53280 | tf_op jit(solution)/shard_map/ppermute | solution.py:404
  15.5 7.8 %collective-permute-done.4.refs_6_.hzm = f32[104,128]{1,0:T(8,128)S(1)} collective-permute-done((f32[104,128]{1,0:T(8,128)S(1)}, f32[104,128]{1,0:T(8,128)S(1)}, u32[]{:S(2)}, u32[]{:S(2)}) %collective-permute-start.4) | collective-permute-done | bytes 53280 | tf_op jit(solution)/shard_map/ppermute | solution.py:404
  25.3 2.9 %collective-permute-start.7 = (f32[768,128]{1,0:T(8,128)S(1)}, f32[768,128]{1,0:T(8,128)S(1)}, u32[]{:S(2)}, u32[]{:S(2)}) collective-permute-start(f32[768,128]{1,0:T(8,128)S(1)} %get-tuple-element.47), channel_id=1, source_target_pairs={{0,96},{32,0},{64,32},{96,64},{1,97},{33,1},{65,33},{97,65},{2,98}... | collective-permute-start | bytes 1179656 | tf_op jit(solution)/shard_map/ppermute | solution.py:404
  29.8 1.7 %collective-permute-start.9 = (f32[384,128]{1,0:T(8,128)S(1)}, f32[384,128]{1,0:T(8,128)S(1)}, u32[]{:S(2)}, u32[]{:S(2)}) collective-permute-start(f32[384,128]{1,0:T(8,128)S(1)} %get-tuple-element.49), channel_id=1, source_target_pairs={{0,24},{8,0},{16,8},{24,16},{1,25},{9,1},{17,9},{25,17},{2,26},{10... | collective-permute-start | bytes 589832 | tf_op jit(solution)/shard_map/ppermute | solution.py:404
  31.5 2.0 %collective-permute-start.11 = (f32[96,128]{1,0:T(8,128)S(1)}, f32[96,128]{1,0:T(8,128)S(1)}, u32[]{:S(2)}, u32[]{:S(2)}) collective-permute-start(f32[96,128]{1,0:T(8,128)S(1)} %get-tuple-element.50), channel_id=1, source_target_pairs={{0,7},{1,0},{2,1},{3,2},{4,3},{5,4},{6,5},{7,6},{8,15},{9,8},{10,9... | collective-permute-start | bytes 147464 | tf_op jit(solution)/shard_map/ppermute | solution.py:404
  33.5 4.1 %collective-permute-done.11.refs_7_.hzp = f32[96,128]{1,0:T(8,128)S(1)} collective-permute-done((f32[96,128]{1,0:T(8,128)S(1)}, f32[96,128]{1,0:T(8,128)S(1)}, u32[]{:S(2)}, u32[]{:S(2)}) %collective-permute-start.11) | collective-permute-done | bytes 49184 | tf_op jit(solution)/shard_map/ppermute | solution.py:404
  37.6 8.2 %collective-permute-done.10.refs_6_.hzm = f32[96,128]{1,0:T(8,128)S(1)} collective-permute-done((f32[96,128]{1,0:T(8,128)S(1)}, f32[96,128]{1,0:T(8,128)S(1)}, u32[]{:S(2)}, u32[]{:S(2)}) %collective-permute-start.10) | collective-permute-done | bytes 49184 | tf_op jit(solution)/shard_map/ppermute | solution.py:404
  46.8 3.2 %collective-permute-start.13 = (f32[768,128]{1,0:T(8,128)S(1)}, f32[768,128]{1,0:T(8,128)S(1)}, u32[]{:S(2)}, u32[]{:S(2)}) collective-permute-start(f32[768,128]{1,0:T(8,128)S(1)} %get-tuple-element.54), channel_id=1, source_target_pairs={{0,96},{32,0},{64,32},{96,64},{1,97},{33,1},{65,33},{97,65},{2,98}... | collective-permute-start | bytes 1179656 | tf_op jit(solution)/shard_map/ppermute | solution.py:404
  53.3 2.0 %collective-permute-start.17 = (f32[96,128]{1,0:T(8,128)S(1)}, f32[96,128]{1,0:T(8,128)S(1)}, u32[]{:S(2)}, u32[]{:S(2)}) collective-permute-start(f32[96,128]{1,0:T(8,128)S(1)} %get-tuple-element.57), channel_id=1, source_target_pairs={{0,7},{1,0},{2,1},{3,2},{4,3},{5,4},{6,5},{7,6},{8,15},{9,8},{10,9... | collective-permute-start | bytes 147464 | tf_op jit(solution)/shard_map/ppermute | solution.py:404
  55.3 2.2 %collective-permute-done.17.refs_7_.hzp = f32[96,128]{1,0:T(8,128)S(1)} collective-permute-done((f32[96,128]{1,0:T(8,128)S(1)}, f32[96,128]{1,0:T(8,128)S(1)}, u32[]{:S(2)}, u32[]{:S(2)}) %collective-permute-start.17) | collective-permute-done | bytes 49184 | tf_op jit(solution)/shard_map/ppermute | solution.py:404
  57.5 8.2 %collective-permute-done.16.refs_6_.hzm = f32[96,128]{1,0:T(8,128)S(1)} collective-permute-done((f32[96,128]{1,0:T(8,128)S(1)}, f32[96,128]{1,0:T(8,128)S(1)}, u32[]{:S(2)}, u32[]{:S(2)}) %collective-permute-start.16) | collective-permute-done | bytes 49184 | tf_op jit(solution)/shard_map/ppermute | solution.py:404
  66.7 3.2 %collective-permute-start.19 = (f32[384,128]{1,0:T(8,128)S(1)}, f32[384,128]{1,0:T(8,128)S(1)}, u32[]{:S(2)}, u32[]{:S(2)}) collective-permute-start(f32[384,128]{1,0:T(8,128)S(1)} %get-tuple-element.62), channel_id=1, source_target_pairs={{0,96},{32,0},{64,32},{96,64},{1,97},{33,1},{65,33},{97,65},{2,98}... | collective-permute-start | bytes 589832 | tf_op jit(solution)/shard_map/ppermute | solution.py:404
  74.5 3.2 %shard_map.60.inside = f32[32,64]{1,0:T(8,128)S(1)} custom-call(f32[46,8,128]{2,1,0:T(8,128)S(1)} %get-tuple-element.42.w_ref, f32[54,8,128]{2,1,0:T(8,128)S(1)} %get-tuple-element.44.d_ref, f32[3,32,2048]{2,1,0:T(8,128)S(1)} %get-tuple-element.58.new_outer.outer, f32[3,32,2048]{2,1,0:T(8,128)S(1)} %get-tuple-element.59.inner), custom_call_target="tpu_custom_call" | custom-call | flops 4000000 | bytes 3000000 | tf_op jit(solution)/shard_map/pallas_call | solution.py:442
  77.7 1.8 %collective-permute-done.21.hzm = f32[96,128]{1,0:T(8,128)S(1)} collective-permute-done((f32[96,128]{1,0:T(8,128)S(1)}, f32[96,128]{1,0:T(8,128)S(1)}, u32[]{:S(2)}, u32[]{:S(2)}) %collective-permute-start.21) | collective-permute-done | bytes 49184 | tf_op jit(solution)/shard_map/ppermute | solution.py:404
  82.1 1.9 %collective-permute-start.25 = (f32[32,128]{1,0:T(8,128)S(1)}, f32[32,128]{1,0:T(8,128)S(1)}, u32[]{:S(2)}, u32[]{:S(2)}) collective-permute-start(f32[32,128]{1,0:T(8,128)S(1)} %add.30), channel_id=1, source_target_pairs={{0,20},{1,21},{2,22},{3,23},{4,16},{5,17},{6,18},{7,19},{8,28},{9,... | collective-permute-start | bytes 49160 | tf_op jit(solution)/shard_map/ppermute | solution.py:435
  84.1 2.6 %collective-permute-start.23 = (f32[32,128]{1,0:T(8,128)S(1)}, f32[32,128]{1,0:T(8,128)S(1)}, u32[]{:S(2)}, u32[]{:S(2)}) collective-permute-start(f32[32,128]{1,0:T(8,128)S(1)} %add.30), channel_id=1, source_target_pairs={{0,4},{1,5},{2,6},{3,7},{4,0},{5,1},{6,2},{7,3},{8,12},{9,13},{10,... | collective-permute-start | bytes 49160 | tf_op jit(solution)/shard_map/ppermute | solution.py:435
  89.4 2.0 %collective-permute-start.27 = (f32[32,128]{1,0:T(8,128)S(1)}, f32[32,128]{1,0:T(8,128)S(1)}, u32[]{:S(2)}, u32[]{:S(2)}) collective-permute-start(f32[32,128]{1,0:T(8,128)S(1)} %add_add_fusion.2), channel_id=1, source_target_pairs={{0,32},{32,64},{64,96},{96,0},{1,33},{33,65},{65,97},{97,1},{2,34}... | collective-permute-start | bytes 49160 | tf_op jit(solution)/shard_map/ppermute | solution.py:435
  94.4 2.2 %collective-permute-done.26 = f32[32,128]{1,0:T(8,128)S(1)} collective-permute-done((f32[32,128]{1,0:T(8,128)S(1)}, f32[32,128]{1,0:T(8,128)S(1)}, u32[]{:S(2)}, u32[]{:S(2)}) %collective-permute-start.26) | collective-permute-done | bytes 16416 | tf_op jit(solution)/shard_map/ppermute | solution.py:435
  96.7 3.6 %collective-permute-start.31 = (f32[32,128]{1,0:T(8,128)S(1)}, f32[32,128]{1,0:T(8,128)S(1)}, u32[]{:S(2)}, u32[]{:S(2)}) collective-permute-start(f32[32,128]{1,0:T(8,128)S(1)} %add_add_fusion.1), channel_id=1, source_target_pairs={{0,3},{1,0},{2,1},{3,2},{4,7},{5,4},{6,5},{7,6},{8,11},{9,8},{10,9... | collective-permute-start | bytes 49160 | tf_op jit(solution)/shard_map/ppermute | solution.py:435
  101.8 3.4 %collective-permute-done.30 = f32[32,128]{1,0:T(8,128)S(1)} collective-permute-done((f32[32,128]{1,0:T(8,128)S(1)}, f32[32,128]{1,0:T(8,128)S(1)}, u32[]{:S(2)}, u32[]{:S(2)}) %collective-permute-start.30) | collective-permute-done | bytes 16416 | tf_op jit(solution)/shard_map/ppermute | solution.py:435
  105.5 3.5 %shard_map.62 = (f32[32,32]{1,0:T(8,128)S(1)}, f32[32,32]{1,0:T(8,128)}) custom-call(f32[32,128]{1,0:T(8,128)S(1)} %add_add_fusion.sums_ref), custom_call_target="tpu_custom_call" | custom-call | flops 4000000 | bytes 3000000 | tf_op jit(solution)/shard_map/pallas_call | solution.py:442
  109.0 2.8 %shard_map.63 = f32[3072,128]{1,0:T(8,128)} custom-call(f32[32,32]{1,0:T(8,128)S(1)} %get-tuple-element.64.mixing_ref, f32[3,32,2048]{2,1,0:T(8,128)S(1)} %get-tuple-element.58.new_outer.outer, f32[3,32,2048]{2,1,0:T(8,128)S(1)} %get-tuple-element.59.inner), custom_call_target="tpu_custom_call" | custom-call | tf_op jit(solution)/shard_map/pallas_call | solution.py:499
  (64 shorter events, 31.1 us)
Async XLA Ops:
  3.3 20.0 %collective-permute-start = (f32[776,128]{1,0:T(8,128)S(1)}, f32[776,128]{1,0:T(8,128)S(1)}, u32[]{:S(2)}, u32[]{:S(2)}) collective-permute-start(f32[776,128]{1,0:T(8,128)S(1)} %get-tuple-element.37), channel_id=1, source_target_pairs={{0,32},{32,64},{64,96},{96,0},{1,33},{33,65},{65,97},{97,1},{2,34}... | collective-permute-start | bytes 1191944 | tf_op jit(solution)/shard_map/ppermute | solution.py:404
  4.9 18.4 %collective-permute-start.1 = (f32[776,128]{1,0:T(8,128)S(1)}, f32[776,128]{1,0:T(8,128)S(1)}, u32[]{:S(2)}, u32[]{:S(2)}) collective-permute-start(f32[776,128]{1,0:T(8,128)S(1)} %get-tuple-element.38), channel_id=1, source_target_pairs={{0,96},{32,0},{64,32},{96,64},{1,97},{33,1},{65,33},{97,65},{2,98}... | collective-permute-start | bytes 1191944 | tf_op jit(solution)/shard_map/ppermute | solution.py:404
  7.6 15.7 %collective-permute-start.2 = (f32[392,128]{1,0:T(8,128)S(1)}, f32[392,128]{1,0:T(8,128)S(1)}, u32[]{:S(2)}, u32[]{:S(2)}) collective-permute-start(f32[392,128]{1,0:T(8,128)S(1)} %get-tuple-element.39), channel_id=1, source_target_pairs={{0,8},{8,16},{16,24},{24,0},{1,9},{9,17},{17,25},{25,1},{2,10},{10... | collective-permute-start | bytes 602120 | tf_op jit(solution)/shard_map/ppermute | solution.py:404
  7.7 15.6 %collective-permute-start.3 = (f32[392,128]{1,0:T(8,128)S(1)}, f32[392,128]{1,0:T(8,128)S(1)}, u32[]{:S(2)}, u32[]{:S(2)}) collective-permute-start(f32[392,128]{1,0:T(8,128)S(1)} %get-tuple-element.40), channel_id=1, source_target_pairs={{0,24},{8,0},{16,8},{24,16},{1,25},{9,1},{17,9},{25,17},{2,26},{10... | collective-permute-start | bytes 602120 | tf_op jit(solution)/shard_map/ppermute | solution.py:404
  9.4 5.8 %collective-permute-start.5 = (f32[104,128]{1,0:T(8,128)S(1)}, f32[104,128]{1,0:T(8,128)S(1)}, u32[]{:S(2)}, u32[]{:S(2)}) collective-permute-start(f32[104,128]{1,0:T(8,128)S(1)} %get-tuple-element.41), channel_id=1, source_target_pairs={{0,7},{1,0},{2,1},{3,2},{4,3},{5,4},{6,5},{7,6},{8,15},{9,8},{10,9... | collective-permute-start | bytes 159752 | tf_op jit(solution)/shard_map/ppermute | solution.py:404
  15.2 8.1 %collective-permute-start.4 = (f32[104,128]{1,0:T(8,128)S(1)}, f32[104,128]{1,0:T(8,128)S(1)}, u32[]{:S(2)}, u32[]{:S(2)}) collective-permute-start(f32[104,128]{1,0:T(8,128)S(1)} %get-tuple-element.41), channel_id=1, source_target_pairs={{0,1},{1,2},{2,3},{3,4},{4,5},{5,6},{6,7},{7,0},{8,9},{9,10},{10,1... | collective-permute-start | bytes 159752 | tf_op jit(solution)/shard_map/ppermute | solution.py:404
  24.9 20.9 %collective-permute-start.6 = (f32[768,128]{1,0:T(8,128)S(1)}, f32[768,128]{1,0:T(8,128)S(1)}, u32[]{:S(2)}, u32[]{:S(2)}) collective-permute-start(f32[768,128]{1,0:T(8,128)S(1)} %get-tuple-element.46), channel_id=1, source_target_pairs={{0,32},{32,64},{64,96},{96,0},{1,33},{33,65},{65,97},{97,1},{2,34}... | collective-permute-start | bytes 1179656 | tf_op jit(solution)/shard_map/ppermute | solution.py:404
  25.3 20.5 %collective-permute-start.7 = (f32[768,128]{1,0:T(8,128)S(1)}, f32[768,128]{1,0:T(8,128)S(1)}, u32[]{:S(2)}, u32[]{:S(2)}) collective-permute-start(f32[768,128]{1,0:T(8,128)S(1)} %get-tuple-element.47), channel_id=1, source_target_pairs={{0,96},{32,0},{64,32},{96,64},{1,97},{33,1},{65,33},{97,65},{2,98}... | collective-permute-start | bytes 1179656 | tf_op jit(solution)/shard_map/ppermute | solution.py:404
  29.7 16.1 %collective-permute-start.8 = (f32[384,128]{1,0:T(8,128)S(1)}, f32[384,128]{1,0:T(8,128)S(1)}, u32[]{:S(2)}, u32[]{:S(2)}) collective-permute-start(f32[384,128]{1,0:T(8,128)S(1)} %get-tuple-element.48), channel_id=1, source_target_pairs={{0,8},{8,16},{16,24},{24,0},{1,9},{9,17},{17,25},{25,1},{2,10},{10... | collective-permute-start | bytes 589832 | tf_op jit(solution)/shard_map/ppermute | solution.py:404
  29.8 16.0 %collective-permute-start.9 = (f32[384,128]{1,0:T(8,128)S(1)}, f32[384,128]{1,0:T(8,128)S(1)}, u32[]{:S(2)}, u32[]{:S(2)}) collective-permute-start(f32[384,128]{1,0:T(8,128)S(1)} %get-tuple-element.49), channel_id=1, source_target_pairs={{0,24},{8,0},{16,8},{24,16},{1,25},{9,1},{17,9},{25,17},{2,26},{10... | collective-permute-start | bytes 589832 | tf_op jit(solution)/shard_map/ppermute | solution.py:404
  31.5 6.1 %collective-permute-start.11 = (f32[96,128]{1,0:T(8,128)S(1)}, f32[96,128]{1,0:T(8,128)S(1)}, u32[]{:S(2)}, u32[]{:S(2)}) collective-permute-start(f32[96,128]{1,0:T(8,128)S(1)} %get-tuple-element.50), channel_id=1, source_target_pairs={{0,7},{1,0},{2,1},{3,2},{4,3},{5,4},{6,5},{7,6},{8,15},{9,8},{10,9... | collective-permute-start | bytes 147464 | tf_op jit(solution)/shard_map/ppermute | solution.py:404
  37.6 8.2 %collective-permute-start.10 = (f32[96,128]{1,0:T(8,128)S(1)}, f32[96,128]{1,0:T(8,128)S(1)}, u32[]{:S(2)}, u32[]{:S(2)}) collective-permute-start(f32[96,128]{1,0:T(8,128)S(1)} %get-tuple-element.50), channel_id=1, source_target_pairs={{0,1},{1,2},{2,3},{3,4},{4,5},{5,6},{6,7},{7,0},{8,9},{9,10},{10,1... | collective-permute-start | bytes 147464 | tf_op jit(solution)/shard_map/ppermute | solution.py:404
  46.7 19.0 %collective-permute-start.12 = (f32[768,128]{1,0:T(8,128)S(1)}, f32[768,128]{1,0:T(8,128)S(1)}, u32[]{:S(2)}, u32[]{:S(2)}) collective-permute-start(f32[768,128]{1,0:T(8,128)S(1)} %get-tuple-element.53), channel_id=1, source_target_pairs={{0,32},{32,64},{64,96},{96,0},{1,33},{33,65},{65,97},{97,1},{2,34}... | collective-permute-start | bytes 1179656 | tf_op jit(solution)/shard_map/ppermute | solution.py:404
  46.8 18.9 %collective-permute-start.13 = (f32[768,128]{1,0:T(8,128)S(1)}, f32[768,128]{1,0:T(8,128)S(1)}, u32[]{:S(2)}, u32[]{:S(2)}) collective-permute-start(f32[768,128]{1,0:T(8,128)S(1)} %get-tuple-element.54), channel_id=1, source_target_pairs={{0,96},{32,0},{64,32},{96,64},{1,97},{33,1},{65,33},{97,65},{2,98}... | collective-permute-start | bytes 1179656 | tf_op jit(solution)/shard_map/ppermute | solution.py:404
  51.5 14.2 %collective-permute-start.14 = (f32[384,128]{1,0:T(8,128)S(1)}, f32[384,128]{1,0:T(8,128)S(1)}, u32[]{:S(2)}, u32[]{:S(2)}) collective-permute-start(f32[384,128]{1,0:T(8,128)S(1)} %get-tuple-element.55), channel_id=1, source_target_pairs={{0,8},{8,16},{16,24},{24,0},{1,9},{9,17},{17,25},{25,1},{2,10},{10... | collective-permute-start | bytes 589832 | tf_op jit(solution)/shard_map/ppermute | solution.py:404
  51.6 14.1 %collective-permute-start.15 = (f32[384,128]{1,0:T(8,128)S(1)}, f32[384,128]{1,0:T(8,128)S(1)}, u32[]{:S(2)}, u32[]{:S(2)}) collective-permute-start(f32[384,128]{1,0:T(8,128)S(1)} %get-tuple-element.56), channel_id=1, source_target_pairs={{0,24},{8,0},{16,8},{24,16},{1,25},{9,1},{17,9},{25,17},{2,26},{10... | collective-permute-start | bytes 589832 | tf_op jit(solution)/shard_map/ppermute | solution.py:404
  57.5 8.2 %collective-permute-start.16 = (f32[96,128]{1,0:T(8,128)S(1)}, f32[96,128]{1,0:T(8,128)S(1)}, u32[]{:S(2)}, u32[]{:S(2)}) collective-permute-start(f32[96,128]{1,0:T(8,128)S(1)} %get-tuple-element.57), channel_id=1, source_target_pairs={{0,1},{1,2},{2,3},{3,4},{4,5},{5,6},{6,7},{7,0},{8,9},{9,10},{10,1... | collective-permute-start | bytes 147464 | tf_op jit(solution)/shard_map/ppermute | solution.py:404
  66.6 12.9 %collective-permute-start.18 = (f32[384,128]{1,0:T(8,128)S(1)}, f32[384,128]{1,0:T(8,128)S(1)}, u32[]{:S(2)}, u32[]{:S(2)}) collective-permute-start(f32[384,128]{1,0:T(8,128)S(1)} %get-tuple-element.61), channel_id=1, source_target_pairs={{0,32},{32,64},{64,96},{96,0},{1,33},{33,65},{65,97},{97,1},{2,34}... | collective-permute-start | bytes 589832 | tf_op jit(solution)/shard_map/ppermute | solution.py:404
  66.7 12.8 %collective-permute-start.19 = (f32[384,128]{1,0:T(8,128)S(1)}, f32[384,128]{1,0:T(8,128)S(1)}, u32[]{:S(2)}, u32[]{:S(2)}) collective-permute-start(f32[384,128]{1,0:T(8,128)S(1)} %get-tuple-element.62), channel_id=1, source_target_pairs={{0,96},{32,0},{64,32},{96,64},{1,97},{33,1},{65,33},{97,65},{2,98}... | collective-permute-start | bytes 589832 | tf_op jit(solution)/shard_map/ppermute | solution.py:404
  71.4 8.0 %collective-permute-start.20 = (f32[384,128]{1,0:T(8,128)S(1)}, f32[384,128]{1,0:T(8,128)S(1)}, u32[]{:S(2)}, u32[]{:S(2)}) collective-permute-start(f32[384,128]{1,0:T(8,128)S(1)} %get-tuple-element.63), channel_id=1, source_target_pairs={{0,8},{8,16},{16,24},{24,0},{1,9},{9,17},{17,25},{25,1},{2,10},{10... | collective-permute-start | bytes 589832 | tf_op jit(solution)/shard_map/ppermute | solution.py:404
  71.5 8.0 %collective-permute-start.21 = (f32[96,128]{1,0:T(8,128)S(1)}, f32[96,128]{1,0:T(8,128)S(1)}, u32[]{:S(2)}, u32[]{:S(2)}) collective-permute-start(f32[96,128]{1,0:T(8,128)S(1)} %get-tuple-element.60.own_ends), channel_id=1, source_target_pairs={{0,1},{1,2},{2,3},{3,4},{4,5},{5,6},{6,7},{7,0},{8,9},{9,10},{10,1... | collective-permute-start | bytes 147464 | tf_op jit(solution)/shard_map/ppermute | solution.py:404
  84.1 5.2 %collective-permute-start.23 = (f32[32,128]{1,0:T(8,128)S(1)}, f32[32,128]{1,0:T(8,128)S(1)}, u32[]{:S(2)}, u32[]{:S(2)}) collective-permute-start(f32[32,128]{1,0:T(8,128)S(1)} %add.30), channel_id=1, source_target_pairs={{0,4},{1,5},{2,6},{3,7},{4,0},{5,1},{6,2},{7,3},{8,12},{9,13},{10,... | collective-permute-start | bytes 49160 | tf_op jit(solution)/shard_map/ppermute | solution.py:435
  91.4 5.2 %collective-permute-start.26 = (f32[32,128]{1,0:T(8,128)S(1)}, f32[32,128]{1,0:T(8,128)S(1)}, u32[]{:S(2)}, u32[]{:S(2)}) collective-permute-start(f32[32,128]{1,0:T(8,128)S(1)} %add_add_fusion.2), channel_id=1, source_target_pairs={{0,64},{32,96},{64,0},{96,32},{1,65},{33,97},{65,1},{97,33},{2,66}... | collective-permute-start | bytes 49160 | tf_op jit(solution)/shard_map/ppermute | solution.py:435
  100.2 5.2 %collective-permute-start.29 = (f32[32,128]{1,0:T(8,128)S(1)}, f32[32,128]{1,0:T(8,128)S(1)}, u32[]{:S(2)}, u32[]{:S(2)}) collective-permute-start(f32[32,128]{1,0:T(8,128)S(1)} %add_add_fusion.1), channel_id=1, source_target_pairs={{0,2},{1,3},{2,0},{3,1},{4,6},{5,7},{6,4},{7,5},{8,10},{9,11},{10,... | collective-permute-start | bytes 49160 | tf_op jit(solution)/shard_map/ppermute | solution.py:435
  (11 other events, 54.9 us)
